TPU v7x, 32 devices: a whole 2x2x4 slice. The times are simulated.
32 devices in a mesh: rows: 4 (over z), feat: 8 (over y, x, core).
Axes of the slice: x: 2, y: 2, z: 4, core: 2. Of those that a mesh axis runs over, the one named last changes fastest.
Arguments:
- codes: int32 [65536, 512], P(('rows', 'feat')), may hold values from 0 to 255, as said below
- node_ids: int32 [2, 65536], P(None, ('rows', 'feat')), may hold values from 0 to 3
- bag_counts: int32 [2, 65536], P(None, ('rows', 'feat')), may hold values from 0 to 3
- labels: int32 [65536], P(('rows', 'feat')), may hold values from 0 to 1
Outputs:
- feature_gain: float32 [2, 4, 512], P(None, None, 'feat')
- node_gain: float32 [2, 4], replicated
Inputs may be any that keep to these rules, and one draw needn't show every extreme that they name: Each feature's codes lie below a cap of that feature; bins above the cap are empty.
All inputs are finite; a program needn't handle non-finite values.
Results may differ from a plain program's by a relative error of at most 0.0003.
Values sent between devices are 32-bit elements; how exact they have to be, the bound alone decides.
A program may use at most 64 MiB of HBM per device.

v0:
```python
import math
import jax
import jax.numpy as jnp
from jax import lax
from jax.sharding import PartitionSpec as P

BINS = 256
CLASSES = 2
TREES = 2
NODES = 4


def make_weights(node_ids, bag_counts, labels):
    trees, count_rows = node_ids.shape
    node_range = jnp.arange(NODES, dtype=jnp.int32)
    class_range = jnp.arange(CLASSES, dtype=jnp.int32)
    node_hit = (node_ids[:, :, None] == node_range).astype(jnp.float32)
    class_hit = (labels[:, None] == class_range).astype(jnp.float32)
    weights = (
        bag_counts.astype(jnp.float32)[:, :, None, None]
        * node_hit[:, :, :, None]
        * class_hit[None, :, None, :]
    )
    return (
        jnp.transpose(weights, (1, 0, 2, 3))
        .reshape(count_rows, trees * NODES * CLASSES)
        .astype(jnp.bfloat16)
    )


def split_gains(left):
    feats = left.shape[0]
    left = left.reshape(feats, TREES, NODES, CLASSES, left.shape[-1])
    total = left[..., -1:]
    n_left = jnp.sum(left, axis=3, keepdims=True)
    n_total = jnp.sum(total, axis=3, keepdims=True)
    n_right = n_total - n_left
    frac = n_left / jnp.maximum(n_total, 1.0)
    spread_terms = (left - total * frac) ** 2
    scaled = n_total / (jnp.maximum(n_left, 1.0) * jnp.maximum(n_right, 1.0))
    spread = jnp.sum(spread_terms * scaled, axis=3)
    best = jnp.max(spread, axis=-1)
    return jnp.transpose(best, (1, 2, 0))


def gains_of(hist):
    bin_index = jnp.arange(BINS, dtype=jnp.int32)
    upper = (bin_index[:, None] <= bin_index[None, :]).astype(jnp.float32)
    left = jnp.einsum("fsb,bk->fsk", hist, upper, precision=lax.Precision.HIGHEST)
    return split_gains(left)


def histogram_of(columns, weights):
    count_rows, count = columns.shape
    block_size = math.gcd(count, 32)
    blocks = jnp.transpose(columns.reshape(count_rows, count // block_size, block_size), (1, 0, 2))
    bin_index = jnp.arange(BINS, dtype=jnp.int32)

    def one_block(column_block):
        onehot = (column_block[:, :, None] == bin_index).astype(jnp.bfloat16)
        return jnp.einsum("rfb,rs->fsb", onehot, weights, preferred_element_type=jnp.float32)

    summed = lax.map(one_block, blocks)
    return summed.reshape(count, weights.shape[1], BINS)


def on_device(codes, node_ids, bag_counts, labels):
    weights = make_weights(node_ids, bag_counts, labels)
    partial_hist = lax.psum_scatter(
        histogram_of(codes, weights), "feat", scatter_dimension=0, tiled=True
    )
    hist = lax.psum(partial_hist, "rows")
    feature_gain = gains_of(hist)
    node_gain = lax.pmax(jnp.max(feature_gain, axis=2), "feat")
    return (feature_gain, node_gain)


def solution(mesh):
    return jax.shard_map(
        on_device,
        mesh=mesh,
        in_specs=(
            P(("rows", "feat"), None),
            P(None, ("rows", "feat")),
            P(None, ("rows", "feat")),
            P(("rows", "feat")),
        ),
        out_specs=(P(None, None, "feat"), P()),
        check_vma=False,
    )
```

profile of v0, /device:TPU:0, one launch (start us, length us, event | category | flops | bytes accessed | tf_op | source)
XLA Modules:
  0.0 460.7 jit_solution(4944158148707824612)
XLA Ops:
  7.2 5.4 %copy.20 = s32[2048,512]{0,1:T(8,128)} copy(s32[2048,512]{1,0:T(8,128)} %param.6) | data formatting | bytes 8388608 | tf_op args[0]
  12.8 286.6 %while.11 = (s32[]{:T(128)}, f32[16,32,16,256]{3,2,1,0:T(8,128)}, s32[16,2048,32]{1,2,0:T(8,128)}, f32[2048,2]{0,1:T(2,128)S(1)}, f32[2048,2,4]{0,2,1:T(4,128)S(1)}, /*index=5*/s32[]{:T(128)}) while((s32[]{:T(128)}, f32[16,32,16,256]{3,2,1,0:T(8,128)}, s32[16,2048,32]{1,2,0:T(8,128)}, f32[2048,2]{0,1:T(2,128)S(1)}, ...), condition=%wide.region_1.2_spmd.clone, body=%wide.region_0.1_spmd.clone.sunk | while | flops 553713664 | bytes 1655369 | solution.py:63
  12.8 1.0 dynamic-slice_bitcast_fusion.2
  13.9 16.8 %fusion.19 = f32[16,32,16,256]{3,2,1,0:T(8,128)} fusion(f32[16,32,16,256]{3,2,1,0:T(8,128)} %get-tuple-element.97, s32[]{:T(128)} %get-tuple-element.96, bf16[2048,16,1]{0,1,2:T(8,128)(2,1)S(1)} %reshape.85, s32[2048,32]{0,1:T(8,128)S(1)} %dynamic-slice_bitcast_fusion.2), kind=kOutput, calls=%fused_computation.6.clone.2 | convolution fusion | flops 553648128 | bytes 852480 | tf_op jit(solution)/shard_map/while/body/eval_jaxpr/rfb,rs->fsb/dot_general | solution.py:61
  30.7 1.0 dynamic-slice_bitcast_fusion.2
  31.8 16.8 %fusion.19 = f32[16,32,16,256]{3,2,1,0:T(8,128)} fusion(f32[16,32,16,256]{3,2,1,0:T(8,128)} %get-tuple-element.97, s32[]{:T(128)} %get-tuple-element.96, bf16[2048,16,1]{0,1,2:T(8,128)(2,1)S(1)} %reshape.85, s32[2048,32]{0,1:T(8,128)S(1)} %dynamic-slice_bitcast_fusion.2), kind=kOutput, calls=%fused_computation.6.clone.2 | convolution fusion | flops 553648128 | bytes 852480 | tf_op jit(solution)/shard_map/while/body/eval_jaxpr/rfb,rs->fsb/dot_general | solution.py:61
  49.7 16.8 %fusion.19 = f32[16,32,16,256]{3,2,1,0:T(8,128)} fusion(f32[16,32,16,256]{3,2,1,0:T(8,128)} %get-tuple-element.97, s32[]{:T(128)} %get-tuple-element.96, bf16[2048,16,1]{0,1,2:T(8,128)(2,1)S(1)} %reshape.85, s32[2048,32]{0,1:T(8,128)S(1)} %dynamic-slice_bitcast_fusion.2), kind=kOutput, calls=%fused_computation.6.clone.2 | convolution fusion | flops 553648128 | bytes 852480 | tf_op jit(solution)/shard_map/while/body/eval_jaxpr/rfb,rs->fsb/dot_general | solution.py:61
  67.6 16.8 %fusion.19 = f32[16,32,16,256]{3,2,1,0:T(8,128)} fusion(f32[16,32,16,256]{3,2,1,0:T(8,128)} %get-tuple-element.97, s32[]{:T(128)} %get-tuple-element.96, bf16[2048,16,1]{0,1,2:T(8,128)(2,1)S(1)} %reshape.85, s32[2048,32]{0,1:T(8,128)S(1)} %dynamic-slice_bitcast_fusion.2), kind=kOutput, calls=%fused_computation.6.clone.2 | convolution fusion | flops 553648128 | bytes 852480 | tf_op jit(solution)/shard_map/while/body/eval_jaxpr/rfb,rs->fsb/dot_general | solution.py:61
  84.4 1.0 dynamic-slice_bitcast_fusion.2
  85.5 16.8 %fusion.19 = f32[16,32,16,256]{3,2,1,0:T(8,128)} fusion(f32[16,32,16,256]{3,2,1,0:T(8,128)} %get-tuple-element.97, s32[]{:T(128)} %get-tuple-element.96, bf16[2048,16,1]{0,1,2:T(8,128)(2,1)S(1)} %reshape.85, s32[2048,32]{0,1:T(8,128)S(1)} %dynamic-slice_bitcast_fusion.2), kind=kOutput, calls=%fused_computation.6.clone.2 | convolution fusion | flops 553648128 | bytes 852480 | tf_op jit(solution)/shard_map/while/body/eval_jaxpr/rfb,rs->fsb/dot_general | solution.py:61
  103.4 16.8 %fusion.19 = f32[16,32,16,256]{3,2,1,0:T(8,128)} fusion(f32[16,32,16,256]{3,2,1,0:T(8,128)} %get-tuple-element.97, s32[]{:T(128)} %get-tuple-element.96, bf16[2048,16,1]{0,1,2:T(8,128)(2,1)S(1)} %reshape.85, s32[2048,32]{0,1:T(8,128)S(1)} %dynamic-slice_bitcast_fusion.2), kind=kOutput, calls=%fused_computation.6.clone.2 | convolution fusion | flops 553648128 | bytes 852480 | tf_op jit(solution)/shard_map/while/body/eval_jaxpr/rfb,rs->fsb/dot_general | solution.py:61
  120.2 1.0 dynamic-slice_bitcast_fusion.2
  121.3 16.8 %fusion.19 = f32[16,32,16,256]{3,2,1,0:T(8,128)} fusion(f32[16,32,16,256]{3,2,1,0:T(8,128)} %get-tuple-element.97, s32[]{:T(128)} %get-tuple-element.96, bf16[2048,16,1]{0,1,2:T(8,128)(2,1)S(1)} %reshape.85, s32[2048,32]{0,1:T(8,128)S(1)} %dynamic-slice_bitcast_fusion.2), kind=kOutput, calls=%fused_computation.6.clone.2 | convolution fusion | flops 553648128 | bytes 852480 | tf_op jit(solution)/shard_map/while/body/eval_jaxpr/rfb,rs->fsb/dot_general | solution.py:61
  138.1 1.0 dynamic-slice_bitcast_fusion.2
  139.2 16.8 %fusion.19 = f32[16,32,16,256]{3,2,1,0:T(8,128)} fusion(f32[16,32,16,256]{3,2,1,0:T(8,128)} %get-tuple-element.97, s32[]{:T(128)} %get-tuple-element.96, bf16[2048,16,1]{0,1,2:T(8,128)(2,1)S(1)} %reshape.85, s32[2048,32]{0,1:T(8,128)S(1)} %dynamic-slice_bitcast_fusion.2), kind=kOutput, calls=%fused_computation.6.clone.2 | convolution fusion | flops 553648128 | bytes 852480 | tf_op jit(solution)/shard_map/while/body/eval_jaxpr/rfb,rs->fsb/dot_general | solution.py:61
  156.1 1.0 dynamic-slice_bitcast_fusion.2
  157.1 16.8 %fusion.19 = f32[16,32,16,256]{3,2,1,0:T(8,128)} fusion(f32[16,32,16,256]{3,2,1,0:T(8,128)} %get-tuple-element.97, s32[]{:T(128)} %get-tuple-element.96, bf16[2048,16,1]{0,1,2:T(8,128)(2,1)S(1)} %reshape.85, s32[2048,32]{0,1:T(8,128)S(1)} %dynamic-slice_bitcast_fusion.2), kind=kOutput, calls=%fused_computation.6.clone.2 | convolution fusion | flops 553648128 | bytes 852480 | tf_op jit(solution)/shard_map/while/body/eval_jaxpr/rfb,rs->fsb/dot_general | solution.py:61
  175.0 16.8 %fusion.19 = f32[16,32,16,256]{3,2,1,0:T(8,128)} fusion(f32[16,32,16,256]{3,2,1,0:T(8,128)} %get-tuple-element.97, s32[]{:T(128)} %get-tuple-element.96, bf16[2048,16,1]{0,1,2:T(8,128)(2,1)S(1)} %reshape.85, s32[2048,32]{0,1:T(8,128)S(1)} %dynamic-slice_bitcast_fusion.2), kind=kOutput, calls=%fused_computation.6.clone.2 | convolution fusion | flops 553648128 | bytes 852480 | tf_op jit(solution)/shard_map/while/body/eval_jaxpr/rfb,rs->fsb/dot_general | solution.py:61
  192.9 16.8 %fusion.19 = f32[16,32,16,256]{3,2,1,0:T(8,128)} fusion(f32[16,32,16,256]{3,2,1,0:T(8,128)} %get-tuple-element.97, s32[]{:T(128)} %get-tuple-element.96, bf16[2048,16,1]{0,1,2:T(8,128)(2,1)S(1)} %reshape.85, s32[2048,32]{0,1:T(8,128)S(1)} %dynamic-slice_bitcast_fusion.2), kind=kOutput, calls=%fused_computation.6.clone.2 | convolution fusion | flops 553648128 | bytes 852480 | tf_op jit(solution)/shard_map/while/body/eval_jaxpr/rfb,rs->fsb/dot_general | solution.py:61
  210.8 16.8 %fusion.19 = f32[16,32,16,256]{3,2,1,0:T(8,128)} fusion(f32[16,32,16,256]{3,2,1,0:T(8,128)} %get-tuple-element.97, s32[]{:T(128)} %get-tuple-element.96, bf16[2048,16,1]{0,1,2:T(8,128)(2,1)S(1)} %reshape.85, s32[2048,32]{0,1:T(8,128)S(1)} %dynamic-slice_bitcast_fusion.2), kind=kOutput, calls=%fused_computation.6.clone.2 | convolution fusion | flops 553648128 | bytes 852480 | tf_op jit(solution)/shard_map/while/body/eval_jaxpr/rfb,rs->fsb/dot_general | solution.py:61
  228.8 16.8 %fusion.19 = f32[16,32,16,256]{3,2,1,0:T(8,128)} fusion(f32[16,32,16,256]{3,2,1,0:T(8,128)} %get-tuple-element.97, s32[]{:T(128)} %get-tuple-element.96, bf16[2048,16,1]{0,1,2:T(8,128)(2,1)S(1)} %reshape.85, s32[2048,32]{0,1:T(8,128)S(1)} %dynamic-slice_bitcast_fusion.2), kind=kOutput, calls=%fused_computation.6.clone.2 | convolution fusion | flops 553648128 | bytes 852480 | tf_op jit(solution)/shard_map/while/body/eval_jaxpr/rfb,rs->fsb/dot_general | solution.py:61
  246.7 16.8 %fusion.19 = f32[16,32,16,256]{3,2,1,0:T(8,128)} fusion(f32[16,32,16,256]{3,2,1,0:T(8,128)} %get-tuple-element.97, s32[]{:T(128)} %get-tuple-element.96, bf16[2048,16,1]{0,1,2:T(8,128)(2,1)S(1)} %reshape.85, s32[2048,32]{0,1:T(8,128)S(1)} %dynamic-slice_bitcast_fusion.2), kind=kOutput, calls=%fused_computation.6.clone.2 | convolution fusion | flops 553648128 | bytes 852480 | tf_op jit(solution)/shard_map/while/body/eval_jaxpr/rfb,rs->fsb/dot_general | solution.py:61
  264.6 16.8 %fusion.19 = f32[16,32,16,256]{3,2,1,0:T(8,128)} fusion(f32[16,32,16,256]{3,2,1,0:T(8,128)} %get-tuple-element.97, s32[]{:T(128)} %get-tuple-element.96, bf16[2048,16,1]{0,1,2:T(8,128)(2,1)S(1)} %reshape.85, s32[2048,32]{0,1:T(8,128)S(1)} %dynamic-slice_bitcast_fusion.2), kind=kOutput, calls=%fused_computation.6.clone.2 | convolution fusion | flops 553648128 | bytes 852480 | tf_op jit(solution)/shard_map/while/body/eval_jaxpr/rfb,rs->fsb/dot_general | solution.py:61
  282.5 16.8 %fusion.19 = f32[16,32,16,256]{3,2,1,0:T(8,128)} fusion(f32[16,32,16,256]{3,2,1,0:T(8,128)} %get-tuple-element.97, s32[]{:T(128)} %get-tuple-element.96, bf16[2048,16,1]{0,1,2:T(8,128)(2,1)S(1)} %reshape.85, s32[2048,32]{0,1:T(8,128)S(1)} %dynamic-slice_bitcast_fusion.2), kind=kOutput, calls=%fused_computation.6.clone.2 | convolution fusion | flops 553648128 | bytes 852480 | tf_op jit(solution)/shard_map/while/body/eval_jaxpr/rfb,rs->fsb/dot_general | solution.py:61
  299.4 74.3 %reduce-scatter.2.cloned.1.call-done = f32[64,16,256]{2,1,0:T(8,128)} async-done(((f32[512,16,256]{2,1,0:T(8,128)}), f32[64,16,256]{2,1,0:T(8,128)}) %reduce-scatter.2.cloned.1.call-update) | async-done | bytes 1048592 | tf_op jit(solution)/shard_map/reduce_scatter | solution.py:69
  373.8 54.3 %all-reduce.2.cloned.1.call-done = f32[64,16,256]{2,1,0:T(8,128)} async-done(((f32[64,16,256]{2,1,0:T(8,128)}), f32[64,16,256]{2,1,0:T(8,128)}) %all-reduce.2.cloned.1.call-update) | async-done | bytes 1048592 | tf_op jit(solution)/shard_map/psum | solution.py:72
  428.0 1.8 fusion.9
  430.5 1.4 fusion.12
  432.1 1.5 reduce_sum.27
  433.6 3.1 copy.28
  437.1 2.0 multiply_reduce_fusion
  439.6 14.3 %pmax.7 = f32[2,4]{1,0:T(2,128)} all-reduce(f32[2,4]{1,0:T(2,128)S(1)} %bitcast_reduce_fusion), channel_id=1, replica_groups=mesh['rows'=4,'feat'=8] {'feat'}, use_global_device_ids=true, to_apply=%region_9.10 | all-reduce | flops 8 | bytes 64 | tf_op jit(solution)/shard_map/pmax | solution.py:74
  (66 shorter events, 12.8 us)
Async XLA Ops:
  7.2 5.5 %copy-start.1 = (s32[2,2048]{1,0:T(2,128)S(1)}, s32[2,2048]{1,0:T(2,128)}, u32[]{:S(2)}) copy-start(s32[2,2048]{1,0:T(2,128)} %param.8) | copy-start | bytes 49156
  7.2 5.5 %copy-start.3 = (s32[2048]{0:T(1024)S(1)}, s32[2048]{0:T(1024)}, u32[]{:S(2)}) copy-start(s32[2048]{0:T(1024)} %param.9) | copy-start | bytes 24580
  7.2 5.5 %copy-start.2 = (s32[2,2048]{1,0:T(2,128)S(1)}, s32[2,2048]{1,0:T(2,128)}, u32[]{:S(2)}) copy-start(s32[2,2048]{1,0:T(2,128)} %param.7) | copy-start | bytes 49156
  7.2 366.5 %reduce-scatter.2.cloned.1.call-start = ((), (), s32[]{:S(2)}) async-start(), calls=%async_computation.1 | async-start | bytes 9437184 | tf_op jit(solution)/shard_map/reduce_scatter | solution.py:69
  299.4 128.7 %all-reduce.2.cloned.1.call-start = ((), (), s32[]{:S(2)}) async-start(), calls=%async_computation.2 | async-start | bytes 2097152 | tf_op jit(solution)/shard_map/psum | solution.py:72
  439.5 14.3 %copy-start = (f32[64,2,4]{0,2,1:T(4,128)}, f32[64,2,4]{0,2,1:T(4,128)S(1)}, u32[]{:S(2)}) copy-start(f32[64,2,4]{0,2,1:T(4,128)S(1)} %copy.26) | copy-start | bytes 6148
Sparse Core Ops, SparseCore 0:
  299.5 74.2 reduce-scatter.1
  376.1 51.8 all-reduce.1
where the time goes:
time: 461 us
  matrix products  271 us (59%)
  waiting for transfers between devices  129 us (28%)
  local copies, waits for them, and re-layouts  25.5 us (6%)
  blocking collectives  14.3 us (3%)
  between operations  14.2 us (3%)
  other arithmetic  6.47 us (1%)
    dot_general x16, matrix products, one_block(): jnp.einsum('rfb,rs->fsb', onehot, weights, preferred_element_type=jnp.flo...  269 us
    reduce_scatter x1, waiting for transfers between devices, on_device(): lax.psum_scatter(histogram_of(codes, weights), 'feat', scatter_dimension=...  74.3 us
    psum x1, waiting for transfers between devices, on_device(): hist = lax.psum(partial_hist, 'rows')  54.3 us
    eq x16, local copies, waits for them, and re-layouts, one_block(): onehot = (column_block[:, :, None] == bin_index).astype(jnp.bfloat16)  15.5 us
    pmax x1, blocking collectives, on_device(): node_gain = lax.pmax(jnp.max(feature_gain, axis=2), 'feat')  14.3 us
  transfers between devices with their start and end apart: 2, of which 2 were waited for; matrix products, arithmetic and copies ran while one was open for 0% of the time, Pallas kernels for 0%

commit v1 on v0

--- a/solution.py
+++ b/solution.py
@@ -8,6 +8,7 @@
 CLASSES = 2
 TREES = 2
 NODES = 4
+supply_spots_up = lambda ax_name, body: jnp.sum(lax.all_gather(body, ax_name), axis=0)
 
 
 def make_weights(node_ids, bag_counts, labels):
@@ -69,7 +70,7 @@
     partial_hist = lax.psum_scatter(
         histogram_of(codes, weights), "feat", scatter_dimension=0, tiled=True
     )
-    hist = lax.psum(partial_hist, "rows")
+    hist = supply_spots_up("rows", partial_hist)
     feature_gain = gains_of(hist)
     node_gain = lax.pmax(jnp.max(feature_gain, axis=2), "feat")
     return (feature_gain, node_gain)

time: 461 us -> 483 us (1.048)
  waiting for transfers between devices: 129 us -> 157 us
    all_gather x0 -> x1, waiting for transfers between devices: none -> 82.3 us  [lax.all_gather(body, ax_name)]
    psum x1 -> x0, waiting for transfers between devices: 54.3 us -> none  [on_device(): hist = lax.psum(partial_hist, 'rows')]
where the time goes in v1:
time: 483 us; the launch traced here: 482 us
  matrix products  270 us (56%)
  waiting for transfers between devices  157 us (33%)
  local copies, waits for them, and re-layouts  22.2 us (5%)
  between operations  14.2 us (3%)
  blocking collectives  14 us (3%)
    dot_general x16, matrix products, one_block(): jnp.einsum('rfb,rs->fsb', onehot, weights, preferred_element_type=jnp.flo...  269 us
    all_gather x1, waiting for transfers between devices, lax.all_gather(body, ax_name)  82.3 us
    reduce_scatter x1, waiting for transfers between devices, on_device(): lax.psum_scatter(histogram_of(codes, weights), 'feat', scatter_dimension=...  74.3 us
    eq x16, local copies, waits for them, and re-layouts, one_block(): onehot = (column_block[:, :, None] == bin_index).astype(jnp.bfloat16)  15.5 us
    pmax x1, blocking collectives, on_device(): node_gain = lax.pmax(jnp.max(feature_gain, axis=2), 'feat')  14 us
  transfers between devices with their start and end apart: 2, of which 2 were waited for; matrix products, arithmetic and copies ran while one was open for 0% of the time, Pallas kernels for 0%

profile of v1, /device:TPU:0, one launch (start us, length us, event | category | flops | bytes accessed | tf_op | source)
XLA Modules:
  0.0 482.3 jit_solution(9039570722934952833)
XLA Ops:
  7.2 5.4 %copy.10 = s32[2048,512]{0,1:T(8,128)} copy(s32[2048,512]{1,0:T(8,128)} %param.6) | data formatting | bytes 8388608 | tf_op args[0]
  12.8 286.6 %while.11 = (s32[]{:T(128)}, f32[16,32,16,256]{3,2,1,0:T(8,128)}, s32[16,2048,32]{1,2,0:T(8,128)}, f32[2048,2]{0,1:T(2,128)S(1)}, f32[2048,2,4]{0,2,1:T(4,128)S(1)}, /*index=5*/s32[]{:T(128)}) while((s32[]{:T(128)}, f32[16,32,16,256]{3,2,1,0:T(8,128)}, s32[16,2048,32]{1,2,0:T(8,128)}, f32[2048,2]{0,1:T(2,128)S(1)}, ...), condition=%wide.region_1.2_spmd.clone, body=%wide.region_0.1_spmd.clone.sunk | while | flops 553713664 | bytes 1655369 | solution.py:64
  12.8 1.0 dynamic-slice_bitcast_fusion.2
  13.9 16.8 %fusion.20 = f32[16,32,16,256]{3,2,1,0:T(8,128)} fusion(f32[16,32,16,256]{3,2,1,0:T(8,128)} %get-tuple-element.99, s32[]{:T(128)} %get-tuple-element.98, bf16[2048,16,1]{0,1,2:T(8,128)(2,1)S(1)} %reshape.84, s32[2048,32]{0,1:T(8,128)S(1)} %dynamic-slice_bitcast_fusion.2), kind=kOutput, calls=%fused_computation.6.clone.2 | convolution fusion | flops 553648128 | bytes 852480 | tf_op jit(solution)/shard_map/while/body/eval_jaxpr/rfb,rs->fsb/dot_general | solution.py:62
  30.7 1.0 dynamic-slice_bitcast_fusion.2
  31.8 16.8 %fusion.20 = f32[16,32,16,256]{3,2,1,0:T(8,128)} fusion(f32[16,32,16,256]{3,2,1,0:T(8,128)} %get-tuple-element.99, s32[]{:T(128)} %get-tuple-element.98, bf16[2048,16,1]{0,1,2:T(8,128)(2,1)S(1)} %reshape.84, s32[2048,32]{0,1:T(8,128)S(1)} %dynamic-slice_bitcast_fusion.2), kind=kOutput, calls=%fused_computation.6.clone.2 | convolution fusion | flops 553648128 | bytes 852480 | tf_op jit(solution)/shard_map/while/body/eval_jaxpr/rfb,rs->fsb/dot_general | solution.py:62
  48.6 1.0 dynamic-slice_bitcast_fusion.2
  49.7 16.8 %fusion.20 = f32[16,32,16,256]{3,2,1,0:T(8,128)} fusion(f32[16,32,16,256]{3,2,1,0:T(8,128)} %get-tuple-element.99, s32[]{:T(128)} %get-tuple-element.98, bf16[2048,16,1]{0,1,2:T(8,128)(2,1)S(1)} %reshape.84, s32[2048,32]{0,1:T(8,128)S(1)} %dynamic-slice_bitcast_fusion.2), kind=kOutput, calls=%fused_computation.6.clone.2 | convolution fusion | flops 553648128 | bytes 852480 | tf_op jit(solution)/shard_map/while/body/eval_jaxpr/rfb,rs->fsb/dot_general | solution.py:62
  66.5 1.0 dynamic-slice_bitcast_fusion.2
  67.6 16.8 %fusion.20 = f32[16,32,16,256]{3,2,1,0:T(8,128)} fusion(f32[16,32,16,256]{3,2,1,0:T(8,128)} %get-tuple-element.99, s32[]{:T(128)} %get-tuple-element.98, bf16[2048,16,1]{0,1,2:T(8,128)(2,1)S(1)} %reshape.84, s32[2048,32]{0,1:T(8,128)S(1)} %dynamic-slice_bitcast_fusion.2), kind=kOutput, calls=%fused_computation.6.clone.2 | convolution fusion | flops 553648128 | bytes 852480 | tf_op jit(solution)/shard_map/while/body/eval_jaxpr/rfb,rs->fsb/dot_general | solution.py:62
  84.4 1.0 dynamic-slice_bitcast_fusion.2
  85.5 16.8 %fusion.20 = f32[16,32,16,256]{3,2,1,0:T(8,128)} fusion(f32[16,32,16,256]{3,2,1,0:T(8,128)} %get-tuple-element.99, s32[]{:T(128)} %get-tuple-element.98, bf16[2048,16,1]{0,1,2:T(8,128)(2,1)S(1)} %reshape.84, s32[2048,32]{0,1:T(8,128)S(1)} %dynamic-slice_bitcast_fusion.2), kind=kOutput, calls=%fused_computation.6.clone.2 | convolution fusion | flops 553648128 | bytes 852480 | tf_op jit(solution)/shard_map/while/body/eval_jaxpr/rfb,rs->fsb/dot_general | solution.py:62
  103.4 16.8 %fusion.20 = f32[16,32,16,256]{3,2,1,0:T(8,128)} fusion(f32[16,32,16,256]{3,2,1,0:T(8,128)} %get-tuple-element.99, s32[]{:T(128)} %get-tuple-element.98, bf16[2048,16,1]{0,1,2:T(8,128)(2,1)S(1)} %reshape.84, s32[2048,32]{0,1:T(8,128)S(1)} %dynamic-slice_bitcast_fusion.2), kind=kOutput, calls=%fused_computation.6.clone.2 | convolution fusion | flops 553648128 | bytes 852480 | tf_op jit(solution)/shard_map/while/body/eval_jaxpr/rfb,rs->fsb/dot_general | solution.py:62
  120.2 1.0 dynamic-slice_bitcast_fusion.2
  121.3 16.8 %fusion.20 = f32[16,32,16,256]{3,2,1,0:T(8,128)} fusion(f32[16,32,16,256]{3,2,1,0:T(8,128)} %get-tuple-element.99, s32[]{:T(128)} %get-tuple-element.98, bf16[2048,16,1]{0,1,2:T(8,128)(2,1)S(1)} %reshape.84, s32[2048,32]{0,1:T(8,128)S(1)} %dynamic-slice_bitcast_fusion.2), kind=kOutput, calls=%fused_computation.6.clone.2 | convolution fusion | flops 553648128 | bytes 852480 | tf_op jit(solution)/shard_map/while/body/eval_jaxpr/rfb,rs->fsb/dot_general | solution.py:62
  138.1 1.0 dynamic-slice_bitcast_fusion.2
  139.2 16.8 %fusion.20 = f32[16,32,16,256]{3,2,1,0:T(8,128)} fusion(f32[16,32,16,256]{3,2,1,0:T(8,128)} %get-tuple-element.99, s32[]{:T(128)} %get-tuple-element.98, bf16[2048,16,1]{0,1,2:T(8,128)(2,1)S(1)} %reshape.84, s32[2048,32]{0,1:T(8,128)S(1)} %dynamic-slice_bitcast_fusion.2), kind=kOutput, calls=%fused_computation.6.clone.2 | convolution fusion | flops 553648128 | bytes 852480 | tf_op jit(solution)/shard_map/while/body/eval_jaxpr/rfb,rs->fsb/dot_general | solution.py:62
  156.1 1.0 dynamic-slice_bitcast_fusion.2
  157.1 16.8 %fusion.20 = f32[16,32,16,256]{3,2,1,0:T(8,128)} fusion(f32[16,32,16,256]{3,2,1,0:T(8,128)} %get-tuple-element.99, s32[]{:T(128)} %get-tuple-element.98, bf16[2048,16,1]{0,1,2:T(8,128)(2,1)S(1)} %reshape.84, s32[2048,32]{0,1:T(8,128)S(1)} %dynamic-slice_bitcast_fusion.2), kind=kOutput, calls=%fused_computation.6.clone.2 | convolution fusion | flops 553648128 | bytes 852480 | tf_op jit(solution)/shard_map/while/body/eval_jaxpr/rfb,rs->fsb/dot_general | solution.py:62
  174.0 1.0 dynamic-slice_bitcast_fusion.2
  175.0 16.8 %fusion.20 = f32[16,32,16,256]{3,2,1,0:T(8,128)} fusion(f32[16,32,16,256]{3,2,1,0:T(8,128)} %get-tuple-element.99, s32[]{:T(128)} %get-tuple-element.98, bf16[2048,16,1]{0,1,2:T(8,128)(2,1)S(1)} %reshape.84, s32[2048,32]{0,1:T(8,128)S(1)} %dynamic-slice_bitcast_fusion.2), kind=kOutput, calls=%fused_computation.6.clone.2 | convolution fusion | flops 553648128 | bytes 852480 | tf_op jit(solution)/shard_map/while/body/eval_jaxpr/rfb,rs->fsb/dot_general | solution.py:62
  192.9 16.8 %fusion.20 = f32[16,32,16,256]{3,2,1,0:T(8,128)} fusion(f32[16,32,16,256]{3,2,1,0:T(8,128)} %get-tuple-element.99, s32[]{:T(128)} %get-tuple-element.98, bf16[2048,16,1]{0,1,2:T(8,128)(2,1)S(1)} %reshape.84, s32[2048,32]{0,1:T(8,128)S(1)} %dynamic-slice_bitcast_fusion.2), kind=kOutput, calls=%fused_computation.6.clone.2 | convolution fusion | flops 553648128 | bytes 852480 | tf_op jit(solution)/shard_map/while/body/eval_jaxpr/rfb,rs->fsb/dot_general | solution.py:62
  210.8 16.8 %fusion.20 = f32[16,32,16,256]{3,2,1,0:T(8,128)} fusion(f32[16,32,16,256]{3,2,1,0:T(8,128)} %get-tuple-element.99, s32[]{:T(128)} %get-tuple-element.98, bf16[2048,16,1]{0,1,2:T(8,128)(2,1)S(1)} %reshape.84, s32[2048,32]{0,1:T(8,128)S(1)} %dynamic-slice_bitcast_fusion.2), kind=kOutput, calls=%fused_computation.6.clone.2 | convolution fusion | flops 553648128 | bytes 852480 | tf_op jit(solution)/shard_map/while/body/eval_jaxpr/rfb,rs->fsb/dot_general | solution.py:62
  228.8 16.8 %fusion.20 = f32[16,32,16,256]{3,2,1,0:T(8,128)} fusion(f32[16,32,16,256]{3,2,1,0:T(8,128)} %get-tuple-element.99, s32[]{:T(128)} %get-tuple-element.98, bf16[2048,16,1]{0,1,2:T(8,128)(2,1)S(1)} %reshape.84, s32[2048,32]{0,1:T(8,128)S(1)} %dynamic-slice_bitcast_fusion.2), kind=kOutput, calls=%fused_computation.6.clone.2 | convolution fusion | flops 553648128 | bytes 852480 | tf_op jit(solution)/shard_map/while/body/eval_jaxpr/rfb,rs->fsb/dot_general | solution.py:62
  246.7 16.8 %fusion.20 = f32[16,32,16,256]{3,2,1,0:T(8,128)} fusion(f32[16,32,16,256]{3,2,1,0:T(8,128)} %get-tuple-element.99, s32[]{:T(128)} %get-tuple-element.98, bf16[2048,16,1]{0,1,2:T(8,128)(2,1)S(1)} %reshape.84, s32[2048,32]{0,1:T(8,128)S(1)} %dynamic-slice_bitcast_fusion.2), kind=kOutput, calls=%fused_computation.6.clone.2 | convolution fusion | flops 553648128 | bytes 852480 | tf_op jit(solution)/shard_map/while/body/eval_jaxpr/rfb,rs->fsb/dot_general | solution.py:62
  264.6 16.8 %fusion.20 = f32[16,32,16,256]{3,2,1,0:T(8,128)} fusion(f32[16,32,16,256]{3,2,1,0:T(8,128)} %get-tuple-element.99, s32[]{:T(128)} %get-tuple-element.98, bf16[2048,16,1]{0,1,2:T(8,128)(2,1)S(1)} %reshape.84, s32[2048,32]{0,1:T(8,128)S(1)} %dynamic-slice_bitcast_fusion.2), kind=kOutput, calls=%fused_computation.6.clone.2 | convolution fusion | flops 553648128 | bytes 852480 | tf_op jit(solution)/shard_map/while/body/eval_jaxpr/rfb,rs->fsb/dot_general | solution.py:62
  281.4 1.0 dynamic-slice_bitcast_fusion.2
  282.5 16.8 %fusion.20 = f32[16,32,16,256]{3,2,1,0:T(8,128)} fusion(f32[16,32,16,256]{3,2,1,0:T(8,128)} %get-tuple-element.99, s32[]{:T(128)} %get-tuple-element.98, bf16[2048,16,1]{0,1,2:T(8,128)(2,1)S(1)} %reshape.84, s32[2048,32]{0,1:T(8,128)S(1)} %dynamic-slice_bitcast_fusion.2), kind=kOutput, calls=%fused_computation.6.clone.2 | convolution fusion | flops 553648128 | bytes 852480 | tf_op jit(solution)/shard_map/while/body/eval_jaxpr/rfb,rs->fsb/dot_general | solution.py:62
  299.4 74.3 %reduce-scatter.2.cloned.1.call-done = f32[64,16,256]{2,1,0:T(8,128)} async-done(((f32[512,16,256]{2,1,0:T(8,128)}), f32[64,16,256]{2,1,0:T(8,128)}) %reduce-scatter.2.cloned.1.call-update) | async-done | bytes 1048592 | tf_op jit(solution)/shard_map/reduce_scatter | solution.py:70
  373.8 82.3 %all-gather.3.cloned.1.call-done = f32[256,16,256]{2,1,0:T(8,128)} async-done(((f32[64,16,256]{2,1,0:T(8,128)}), f32[256,16,256]{2,1,0:T(8,128)}) %all-gather.3.cloned.1.call-update) | async-done | bytes 4194320 | tf_op jit(solution)/shard_map/all_gather | solution.py:11
  456.1 2.8 reduce_sum.36
  461.4 14.0 %pmax.7 = f32[2,4]{1,0:T(2,128)} all-reduce(f32[2,4]{1,0:T(2,128)S(1)} %bitcast_reduce_fusion), channel_id=1, replica_groups=mesh['rows'=4,'feat'=8] {'feat'}, use_global_device_ids=true, to_apply=%region_9.10 | all-reduce | flops 8 | bytes 64 | tf_op jit(solution)/shard_map/pmax | solution.py:75
  (64 shorter events, 9.8 us)
Async XLA Ops:
  7.2 5.5 %copy-start.1 = (s32[2,2048]{1,0:T(2,128)S(1)}, s32[2,2048]{1,0:T(2,128)}, u32[]{:S(2)}) copy-start(s32[2,2048]{1,0:T(2,128)} %param.8) | copy-start | bytes 49156
  7.2 5.5 %copy-start.3 = (s32[2048]{0:T(1024)S(1)}, s32[2048]{0:T(1024)}, u32[]{:S(2)}) copy-start(s32[2048]{0:T(1024)} %param.9) | copy-start | bytes 24580
  7.2 5.5 %copy-start.2 = (s32[2,2048]{1,0:T(2,128)S(1)}, s32[2,2048]{1,0:T(2,128)}, u32[]{:S(2)}) copy-start(s32[2,2048]{1,0:T(2,128)} %param.7) | copy-start | bytes 49156
  7.2 366.5 %reduce-scatter.2.cloned.1.call-start = ((), (), s32[]{:S(2)}) async-start(), calls=%async_computation.1 | async-start | bytes 9437184 | tf_op jit(solution)/shard_map/reduce_scatter | solution.py:70
  299.4 156.7 %all-gather.3.cloned.1.call-start = ((), (), s32[]{:S(2)}) async-start(), calls=%async_computation.2 | async-start | bytes 5242880 | tf_op jit(solution)/shard_map/all_gather | solution.py:11
  461.3 14.1 %copy-start = (f32[64,2,4]{0,2,1:T(4,128)}, f32[64,2,4]{0,2,1:T(4,128)S(1)}, u32[]{:S(2)}) copy-start(f32[64,2,4]{0,2,1:T(4,128)S(1)} %reduce_max.18) | copy-start | bytes 6148
Sparse Core Ops, SparseCore 0:
  299.5 74.2 reduce-scatter.1
  375.3 80.7 all-gather.2
